TPU v7x, 128 devices: a whole 4x4x4 slice. The times are simulated.
128 devices in a mesh: rows: 16 (over z, x), grid: 8 (over y, core).
Axes of the slice: x: 4, y: 4, z: 4, core: 2. Of those that a mesh axis runs over, the one named last changes fastest.
Arguments:
- design: bfloat16 [393216, 1024], P(('rows', 'grid')), may hold values from -24 to 24
- observed: float32 [393216], P(('rows', 'grid')), may hold values from -6 to 6
- weight_class: int32 [393216], P(('rows', 'grid')), may hold values from 0 to 15
- calib_unit: int32 [393216], P(('rows', 'grid')), may hold values from 0 to 63
- class_weight: float32 [16], replicated, may hold values from 0.5 to 8
- calib_scale: float32 [64, 8], replicated, may hold values from 0.5 to 2
Outputs:
- normal_matrix: float32 [1024, 1024], P('rows', 'grid')
- right_hand: float32 [1024], P(('rows', 'grid'))
- chi_square: float32 [], replicated
All inputs are finite; a program needn't handle non-finite values.
Results may differ from a plain program's by a relative error of at most 0.01.
Values sent between devices are 32-bit elements; how exact they have to be, the bound alone decides.
A program may use at most 64 MiB of HBM per device.

v0:
```python
import functools

import jax
import jax.numpy as jnp
from jax import lax
from jax.sharding import Mesh
from jax.sharding import PartitionSpec as P

ROWS = ("rows_0", "rows_1")
GRID = ("grid_0", "grid_1")
ROWS_GRID = ("rows_0", "rows_1", "grid_0", "grid_1")


def cut_along(shard, dim, length):
    lengths = shard.shape
    blocks = shard.reshape(*lengths[:dim], length, lengths[dim] // length, *lengths[dim + 1 :])
    return jnp.moveaxis(blocks, dim, 0)


def summed_on_arrival(shard, axis, dim):
    blocks = cut_along(shard, dim, lax.axis_size(axis))
    arrived = lax.all_to_all(blocks, axis, split_axis=0, concat_axis=0, tiled=True)
    return arrived.sum(axis=0)


def sum_by_axis(shard, axes, dim):
    far, near = axes
    blocks = cut_along(shard, dim, lax.axis_size(far))
    nearer = summed_on_arrival(blocks, near, dim + 1)
    arrived = lax.all_to_all(nearer, far, split_axis=0, concat_axis=0, tiled=True)
    return arrived.sum(axis=0)


def by_axis(shard, axes):
    return functools.reduce(lax.psum, axes, shard)


def local(design, observed, weight_class, calib_unit, class_weight, calib_scale):
    row_count = design.shape[0]
    width = design.shape[1]
    blocks = calib_scale.shape[1]
    block_width = width // blocks
    count_rows = lax.axis_size(ROWS)
    count_grid = lax.axis_size(GRID)
    total_rows = row_count * count_rows * count_grid
    class_hot = (
        weight_class[:, None] == jnp.arange(class_weight.shape[0], dtype=jnp.int32)[None, :]
    ).astype(jnp.float32)
    row_weight = jnp.dot(class_hot, class_weight, precision=lax.Precision.HIGHEST)
    root_weight = jnp.sqrt(row_weight)
    unit_hot = (
        calib_unit[:, None] == jnp.arange(calib_scale.shape[0], dtype=jnp.int32)[None, :]
    ).astype(jnp.float32)
    row_scales = jnp.dot(unit_hot, calib_scale, precision=lax.Precision.HIGHEST)
    scaled = (
        (
            design.reshape(row_count, blocks, block_width).astype(jnp.float32)
            * row_scales[:, :, None]
        )
        .reshape(row_count, width)
        .astype(jnp.bfloat16)
    )
    weighted = (root_weight[:, None] * scaled.astype(jnp.float32)).astype(jnp.bfloat16)
    band = width // count_rows
    panel = width // count_grid
    term = jnp.einsum(
        "nra,ngb->rgab",
        weighted.reshape(row_count, count_rows, band),
        weighted.reshape(row_count, count_grid, panel),
        preferred_element_type=jnp.float32,
    )
    term = term.reshape(count_rows * count_grid * band, panel)
    gram = sum_by_axis(term, (("rows_0", "rows_1", "grid_0"), "grid_1"), 0)
    weighted_obs = (root_weight * observed).astype(jnp.bfloat16)
    rhs_term = jnp.dot(weighted_obs, weighted, preferred_element_type=jnp.float32)
    chi_term = jnp.sum(row_weight * observed * observed)
    joined_terms = jnp.concatenate([rhs_term, chi_term[None]], axis=0)
    summed_small = by_axis(joined_terms, ROWS_GRID)
    share = width // (count_rows * count_grid)
    device_index = lax.axis_index(ROWS) * count_grid + lax.axis_index(GRID)
    right_hand = lax.dynamic_slice_in_dim(summed_small, device_index * share, share, 0)
    chi_total = summed_small[width]
    return (gram / total_rows, right_hand / total_rows, chi_total / total_rows)


def solution(mesh):
    finer = Mesh(mesh.devices.reshape(4, 4, 4, 2), ("rows_0", "rows_1", "grid_0", "grid_1"))
    return jax.shard_map(
        local,
        mesh=finer,
        in_specs=(P(ROWS_GRID, None), P(ROWS_GRID), P(ROWS_GRID), P(ROWS_GRID), P(), P()),
        out_specs=(P(ROWS, GRID), P(ROWS_GRID), P()),
        check_vma=False,
    )
```

profile of v0, /device:TPU:0, one launch (start us, length us, event | category | flops | bytes accessed | tf_op | source)
XLA Modules:
  0.0 104.4 jit_solution(11339476915479453611)
XLA Ops:
  0.6 0.0 copy-start
  0.6 0.0 copy-start.5
  0.7 0.0 copy-start.3
  0.7 0.0 copy-start.2
  0.7 0.0 copy-start.4
  0.7 8.7 %copy.19 = bf16[3072,1024]{0,1:T(8,128)(2,1)} copy(bf16[3072,1024]{1,0:T(8,128)(2,1)} %param.6) | data formatting | bytes 12582912 | tf_op args[0]
  9.4 0.0 copy-done.5
  9.4 0.0 copy-done.3
  9.4 0.2 fusion.3
  9.6 0.0 copy-done.2
  9.6 0.6 multiply_convert_fusion.1
  10.2 0.0 copy-done
  10.2 0.0 copy-done.4
  10.2 2.3 %fusion.1 = f32[3072,8]{0,1:T(8,128)S(1)} fusion(f32[64,8]{0,1:T(8,128)S(1)} %copy-done, s32[3072]{0:T(1024)S(1)} %copy-done.4), kind=kOutput, calls=%fused_computation.5 | convolution fusion | flops 19070976 | bytes 112640 | tf_op jit(solution)/shard_map/dot_general | solution.py:54
  12.5 4.5 %multiply_convert_fusion = bf16[3072,1024]{0,1:T(8,128)(2,1)S(1)} fusion(bf16[3072,1024]{0,1:T(8,128)(2,1)} %copy.19, f32[3072,8]{0,1:T(8,128)S(1)} %fusion.1, f32[3072]{0:T(1024)S(1)} %get-tuple-element.5), kind=kLoop, calls=%fused_computation.2 | loop fusion | flops 18874368 | bytes 12693504 | tf_op jit(solution)/shard_map/convert_element_type | solution.py:63
  17.1 0.0 copy-start.1
  17.1 6.7 %convolution_bitcast_fusion = f32[16,8,64,128]{3,2,0,1:T(8,128)S(1)} fusion(bf16[3072,8,128,1]{0,2,3,1:T(8,128)(2,1)S(1)} %bitcast.31, bf16[3072,16,64,1]{0,2,1,3:T(8,128)(2,1)S(1)} %bitcast.32), kind=kOutput, calls=%fused_computation.3 | convolution fusion | flops 6442450944 | bytes 16777216 | tf_op jit(solution)/shard_map/nra,ngb->rgab/dot_general | solution.py:66
  23.8 0.0 copy-done.1
  23.8 0.6 copy.21
  24.4 0.6 copy.22
  24.9 8.2 %all_to_all.10 = f32[2,64,64,128]{3,2,1,0:T(8,128)} all-to-all(f32[2,64,64,128]{3,2,1,0:T(8,128)S(1)} %copy.22), channel_id=1, replica_groups=mesh['rows_0'=4,'rows_1'=4,'grid_0'=4,'grid_1'=2] {'grid_1'}, dimensions={0} | all-to-all | bytes 8388608 | tf_op jit(solution)/shard_map/all_to_all | solution.py:22
  33.1 4.1 %reduce_sum.27 = f32[64,64,128]{2,1,0:T(8,128)} reduce(f32[2,64,64,128]{3,2,1,0:T(8,128)} %all_to_all.10, f32[]{:T(128)} %constant.11.clone.1), dimensions={0}, to_apply=%region_0.0 | reduce | flops 524288 | bytes 6291460 | tf_op jit(solution)/shard_map/reduce_sum | solution.py:23
  37.2 11.5 %all-to-all-start.1 = ((f32[64,64,128]{2,1,0:T(8,128)}), f32[64,64,128]{2,1,0:T(8,128)S(1)}, u32[]{:S(2)}, u32[]{:S(2)}) async-start(f32[64,64,128]{2,1,0:T(8,128)} %reduce_sum.27), calls=%async_computation.1 | async-start | bytes 4194304 | tf_op jit(solution)/shard_map/all_to_all | solution.py:30
  48.8 4.5 %fusion.7 = f32[1,1024]{1,0:T(1,128)S(1)} fusion(bf16[3072,1]{0,1:T(2,128)(2,1)S(1)} %reshape.27, bf16[3072,1024]{0,1:T(8,128)(2,1)} %copy-done.1), kind=kOutput, calls=%fused_computation.17 | convolution fusion | flops 6291456 | bytes 6301696 | tf_op jit(solution)/shard_map/dot_general | solution.py:75
  53.3 0.7 pad_maximum_fusion
  53.9 23.9 %psum.28 = f32[1025]{0:T(1024)S(1)} all-reduce(f32[1025]{0:T(1024)S(1)} %pad_maximum_fusion), channel_id=1, replica_groups=mesh['rows_0'=4,'rows_1'=4,'grid_0'=4,'grid_1'=2] {'rows_0'}, use_global_device_ids=true, to_apply=%region_3.0 | all-reduce | flops 1025 | bytes 8200 | tf_op jit(solution)/shard_map/psum | solution.py:35
  77.8 10.3 %psum.29 = f32[1025]{0:T(1024)S(1)} all-reduce(f32[1025]{0:T(1024)S(1)} %psum.28), channel_id=1, replica_groups=mesh['rows_0'=4,'rows_1'=4,'grid_0'=4,'grid_1'=2] {'rows_1'}, use_global_device_ids=true, to_apply=%region_4.0 | all-reduce | flops 1025 | bytes 8200 | tf_op jit(solution)/shard_map/psum | solution.py:35
  88.2 10.1 %psum.30 = f32[1025]{0:T(1024)S(1)} all-reduce(f32[1025]{0:T(1024)S(1)} %psum.29), channel_id=1, replica_groups=mesh['rows_0'=4,'rows_1'=4,'grid_0'=4,'grid_1'=2] {'grid_0'}, use_global_device_ids=true, to_apply=%region_5.0 | all-reduce | flops 1025 | bytes 8200 | tf_op jit(solution)/shard_map/psum | solution.py:35
  98.3 2.5 %psum.31 = f32[1025]{0:T(1024)S(1)} all-reduce(f32[1025]{0:T(1024)S(1)} %psum.30), channel_id=1, replica_groups=mesh['rows_0'=4,'rows_1'=4,'grid_0'=4,'grid_1'=2] {'grid_1'}, use_global_device_ids=true, to_apply=%region_6.0 | all-reduce | flops 1025 | bytes 8200 | tf_op jit(solution)/shard_map/psum | solution.py:35
  100.8 0.5 slice.4
  102.0 0.6 dynamic-slice_multiply_fusion
  102.5 0.0 all-to-all-done.1
  102.6 0.1 reduce_sum.28
  102.7 0.6 broadcast_multiply_fusion
  (1 shorter events, 0.0 us)
Async XLA Ops:
  0.6 9.5 %copy-start = (f32[64,8]{0,1:T(8,128)S(1)}, f32[64,8]{0,1:T(8,128)}, u32[]{:S(2)}) copy-start(f32[64,8]{0,1:T(8,128)} %param.11) | copy-start | bytes 6148
  0.6 8.7 %copy-start.5 = (f32[16]{0:T(128)S(1)}, f32[16]{0:T(128)}, u32[]{:S(2)}) copy-start(f32[16]{0:T(128)} %param.10) | copy-start | bytes 196
  0.7 8.7 %copy-start.3 = (s32[3072]{0:T(1024)S(1)}, s32[3072]{0:T(1024)}, u32[]{:S(2)}) copy-start(s32[3072]{0:T(1024)} %param.8) | copy-start | bytes 36868
  0.7 8.9 %copy-start.2 = (f32[3072]{0:T(1024)S(1)}, f32[3072]{0:T(1024)}, u32[]{:S(2)}) copy-start(f32[3072]{0:T(1024)} %param.7) | copy-start | bytes 36868
  0.7 9.5 %copy-start.4 = (s32[3072]{0:T(1024)S(1)}, s32[3072]{0:T(1024)}, u32[]{:S(2)}) copy-start(s32[3072]{0:T(1024)} %param.9) | copy-start | bytes 36868
  17.1 6.7 %copy-start.1 = (bf16[3072,1024]{0,1:T(8,128)(2,1)}, bf16[3072,1024]{0,1:T(8,128)(2,1)S(1)}, u32[]{:S(2)}) copy-start(bf16[3072,1024]{0,1:T(8,128)(2,1)S(1)} %multiply_convert_fusion) | copy-start | bytes 18874372
  37.2 65.4 %all-to-all-start.1 = ((f32[64,64,128]{2,1,0:T(8,128)}), f32[64,64,128]{2,1,0:T(8,128)S(1)}, u32[]{:S(2)}, u32[]{:S(2)}) async-start(f32[64,64,128]{2,1,0:T(8,128)} %reduce_sum.27), calls=%async_computation.1 | async-start | bytes 4194304 | tf_op jit(solution)/shard_map/all_to_all | solution.py:30
where the time goes:
time: 106 us; the launch traced here: 104 us
  blocking collectives  55 us (52%)
  matrix products  13.7 us (13%)
  starting transfers between devices  11.5 us (11%)
  other arithmetic  11.2 us (11%)
  local copies, waits for them, and re-layouts  10.4 us (10%)
  between operations  2.57 us (2%)
    psum x4, blocking collectives, by_axis(): return functools.reduce(lax.psum, axes, shard)  46.8 us
    all_to_all x1, starting transfers between devices, sum_by_axis(): lax.all_to_all(nearer, far, split_axis=0, concat_axis=0, tiled=True)  11.5 us
    unnamed x13, local copies, waits for them, and re-layouts  8.71 us
    all_to_all x1, blocking collectives, summed_on_arrival(): lax.all_to_all(blocks, axis, split_axis=0, concat_axis=0, tiled=True)  8.17 us
    dot_general x1, matrix products, local(): jnp.einsum('nra,ngb->rgab', weighted.reshape(row_count, count_rows, band)...  6.69 us
    convert_element_type x1, other arithmetic, local(): (root_weight[:, None] * scaled.astype(jnp.float32)).astype(jnp.bfloat16)  4.54 us
    dot_general x1, matrix products, local(): jnp.dot(weighted_obs, weighted, preferred_element_type=jnp.float32)  4.5 us
    reduce_sum x1, other arithmetic, summed_on_arrival(): return arrived.sum(axis=0)  4.08 us
  transfers between devices with their start and end apart: 1, of which 0 were waited for; matrix products, arithmetic and copies ran while one was open for 6% of the time, Pallas kernels for 0%

commit v1 on v0

v1 whole, which is shorter than its diff:
```python
import functools

import jax
import jax.numpy as jnp
from jax import lax
from jax.experimental import pallas as pl
from jax.experimental.pallas import tpu as pltpu
from jax.sharding import PartitionSpec as P

F32 = jnp.float32
BF16 = jnp.bfloat16
ROWS = 3072
WIDTH = 1024
BLOCKS = 8
LANES = 128
UNITS = 64
CLASSES = 16
CHUNK = 256
CHUNKS = ROWS // CHUNK
TILE = 72
PART = 24
TOTAL = 393216.0
OFFSETS = (2, 1, 3, 0)
NT = (((1,), (1,)), ((), ()))
MESH = pl.DeviceIdType.MESH


def part_rows(part):
    return pl.ds(PART * part, PART)


def kernel(
    design, observed, weight_class, calib_unit, class_weight, scale_t,
    out,
    dbuf, wt, row_scale, row_obs, own, other, arrived,
    ring_x, ring_z, ring_y, ring_2, last,
    load_sem, send_sem, recv_sem,
):
    r = lax.axis_index("rows")
    g = lax.axis_index("grid")
    z, x, y, c = r // 4, r % 4, g // 2, g % 2

    for q in range(CHUNKS):
        rows = pl.ds(q * CHUNK, CHUNK)
        pltpu.make_async_copy(design.at[rows], dbuf.at[rows], load_sem.at[q]).start()

    def device(dz=0, dx=0, dy=0, flip=False):
        core = 1 - c if flip else c
        return (4 * ((z + dz) % 4) + (x + dx) % 4, 2 * ((y + dy) % 4) + core)

    partner = device(flip=True)
    axis_device = {
        "x": lambda d: device(dx=d),
        "z": lambda d: device(dz=d),
        "y": lambda d: device(dy=d),
    }
    barrier = pltpu.get_barrier_semaphore()
    peers = [partner] + [axis_device[a](d) for a in "xzy" for d in (1, 2, 3)]
    for peer in peers:
        pl.semaphore_signal(barrier, inc=1, device_id=peer, device_id_type=MESH)

    started = []

    def send(src, dst, peer):
        index = len(started)
        copy = pltpu.make_async_remote_copy(
            src_ref=src, dst_ref=dst, send_sem=send_sem.at[index],
            recv_sem=recv_sem.at[index], device_id=peer, device_id_type=MESH,
        )
        copy.start()
        started.append(copy)
        return copy

    classes = weight_class[...]
    row_weight = jnp.zeros(classes.shape, F32)
    for k in range(CLASSES):
        row_weight = jnp.where(classes == k, class_weight[k], row_weight)
    root = jnp.sqrt(row_weight)
    obs = observed[...]
    chi = jnp.sum(row_weight * obs * obs)
    root_obs = root * obs
    unit_id = lax.broadcasted_iota(jnp.int32, (UNITS, LANES), 0)
    scales = scale_t[...]
    for q in range(ROWS // LANES):
        cols = slice(q * LANES, (q + 1) * LANES)
        hot = (unit_id == calib_unit[q : q + 1, :]).astype(F32)
        scale = jnp.dot(scales, hot, precision=lax.Precision.HIGHEST, preferred_element_type=F32)
        scale = scale * root[q : q + 1, :]
        row_scale[:, cols] = scale
        value = scale * root_obs[q : q + 1, :]
        high = value.astype(BF16)
        low = (value - high.astype(F32)).astype(BF16)
        row_obs[:, cols] = jnp.concatenate([high, low], axis=0)

    def block_at(position):
        group, a = position // 2, position % 2
        k = 2 * (group // 2) + a
        core = c if group % 2 else 1 - c
        return (y + OFFSETS[k]) % 4, core

    def load_chunk(q, acc):
        rows = pl.ds(pl.multiple_of(q * CHUNK, CHUNK), CHUNK)
        pltpu.make_async_copy(design.at[rows], dbuf.at[rows], load_sem.at[q]).wait()
        for position in range(BLOCKS):
            high, core = block_at(position)
            block = 2 * high + core
            cols = pl.ds(pl.multiple_of(block * LANES, LANES), LANES)
            piece = dbuf[rows, cols].T.astype(F32)
            wt[position, :, rows] = (piece * row_scale[pl.ds(block, 1), rows]).astype(BF16)
        return acc + jnp.dot(row_obs[:, rows], dbuf[rows, :], preferred_element_type=F32)

    sums = lax.fori_loop(0, CHUNKS, load_chunk, jnp.zeros((2 * BLOCKS, WIDTH), F32))
    sums = sums[:BLOCKS] + sums[BLOCKS:]
    line = lax.broadcasted_iota(jnp.int32, (8, LANES), 0)
    for block in range(BLOCKS):
        rhs = sums[block : block + 1, block * LANES : (block + 1) * LANES]
        extra = jnp.where(line == 0, rhs, jnp.where(line == 1, chi, 0.0))
        for k in range(4):
            for half in range(2):
                strip = 2 * (block % 2) + half
                own[k, block // 2, strip, 64:72, :] = extra
                other[k, block // 2, strip, 64:72, :] = extra

    def store(row_position, col_position, value):
        group, a = col_position // 2, col_position % 2
        target = own if group % 2 else other
        k = 2 * (group // 2) + a
        high, core = block_at(row_position)
        for half in range(2):
            target[k, high, 2 * core + half, 0:64, :] = value[64 * half : 64 * half + 64]

    def panel(group):
        right = wt[2 * group : 2 * group + 2].reshape(2 * LANES, ROWS)
        count = BLOCKS - 2 * group
        left = wt[2 * group : BLOCKS].reshape(count * LANES, ROWS)
        product = lax.dot_general(left, right, NT, preferred_element_type=F32)
        for i in range(count):
            for a in range(2):
                value = product[i * LANES : (i + 1) * LANES, a * LANES : (a + 1) * LANES]
                store(2 * group + i, 2 * group + a, value)
                if i >= 2:
                    store(2 * group + a, 2 * group + i, value.T)

    def exchange(pair):
        return [send(other.at[k], arrived.at[k], partner) for k in (2 * pair, 2 * pair + 1)]

    def merge(pair, copies):
        for copy in copies:
            copy.wait_recv()
        for k in (2 * pair, 2 * pair + 1):
            def add(i, _):
                own[k, i // 4, i % 4] = own[k, i // 4, i % 4] + arrived[k, i // 4, i % 4]
                return 0
            lax.fori_loop(0, 16, add, 0)

    class Ring:
        def __init__(self, axis, src, bufs):
            self.right, self.left = axis_device[axis](1), axis_device[axis](3)
            self.src, self.bufs = src, bufs

        def start_far(self):
            self.hop_a = send(self.src(2, 0), self.bufs[0], self.right)
            self.hop_b = send(self.src(2, 1), self.bufs[1], self.left)

        def start_right(self):
            self.direct_b = send(self.src(1, 1), self.bufs[3], self.right)

        def start_left(self):
            self.direct_a = send(self.src(3, 0), self.bufs[2], self.left)

        def mid_a(self):
            self.hop_a.wait_recv()
            self.bufs[0][...] = self.bufs[0][...] + self.src(1, 0)[...]
            self.last_a = send(self.bufs[0], self.bufs[4], self.right)

        def mid_b(self):
            self.hop_b.wait_recv()
            self.bufs[1][...] = self.bufs[1][...] + self.src(3, 1)[...]
            self.last_b = send(self.bufs[1], self.bufs[5], self.left)

        def start(self):
            self.start_far()
            self.start_right()
            self.start_left()

        def mid(self):
            self.mid_a()
            self.mid_b()

        def finish(self):
            self.direct_a.wait_recv()
            self.last_a.wait_recv()
            mine = self.src(0, 0)
            mine[...] = mine[...] + self.bufs[2][...] + self.bufs[4][...]
            self.direct_b.wait_recv()
            self.last_b.wait_recv()
            mine = self.src(0, 1)
            mine[...] = mine[...] + self.bufs[3][...] + self.bufs[5][...]

    panel_of = {2: 0, 1: 1, 3: 2, 0: 3}

    def first_x(pair):
        def src(d, half):
            return own.at[2 * pair + half, :, (x + d) % 4, part_rows(0), :]
        return Ring("x", src, [ring_x.at[pair, i] for i in range(6)])

    def first_z(pair):
        def src(d, half):
            return own.at[2 * pair + half, (z + d) % 4, :, part_rows(2), :]
        return Ring("z", src, [ring_z.at[pair, i] for i in range(6)])

    def first_y():
        def src(d, half):
            return own.at[panel_of[d], pl.ds(2 * half, 2), :, part_rows(1), :]
        return Ring("y", src, [ring_y.at[i] for i in range(6)])

    def second(part):
        def src(d, half):
            two = pl.ds(2 * half, 2)
            if part == 0:
                return own.at[panel_of[d], two, x, part_rows(0), :]
            if part == 1:
                return own.at[3, (z + d) % 4, two, part_rows(1), :]
            return own.at[two, z, (x + d) % 4, part_rows(2), :]
        return Ring("yzx"[part], src, [ring_2.at[part, i] for i in range(6)])

    def third_src(part, d):
        if part == 0:
            return own.at[3, (z + d) % 4, x, part_rows(0), :]
        if part == 1:
            return own.at[3, z, (x + d) % 4, part_rows(1), :]
        return own.at[panel_of[d], z, x, part_rows(2), :]

    def third(part):
        to = axis_device["zxy"[part]]
        return [send(third_src(part, d), last.at[part, d - 1], to(d)) for d in (2, 1, 3)]

    def third_finish(part, copies):
        for copy in copies:
            copy.wait_recv()
        total = third_src(part, 0)[...] + last[part, 0] + last[part, 1] + last[part, 2]
        out[part_rows(part), :] = total * (1.0 / TOTAL)

    pl.semaphore_wait(barrier, len(peers))
    panel(0)
    pair_0 = exchange(0)
    panel(1)
    merge(0, pair_0)
    x_0, z_0, y_all = first_x(0), first_z(0), first_y()
    x_0.start()
    z_0.start()
    y_all.start_far()
    y_all.start_right()
    panel(2)
    pair_1 = exchange(1)
    panel(3)
    merge(1, pair_1)
    x_1, z_1 = first_x(1), first_z(1)
    x_1.start()
    z_1.start()
    y_all.start_left()
    x_0.mid()
    z_0.mid()
    y_all.mid()
    x_1.mid()
    z_1.mid()
    rings = [second(part) for part in range(3)]
    y_all.finish()
    rings[1].start()
    x_0.finish()
    x_1.finish()
    rings[0].start()
    z_0.finish()
    z_1.finish()
    rings[2].start()
    for part in (1, 0, 2):
        rings[part].mid()
    tails = {}
    for part in (1, 0, 2):
        rings[part].finish()
        tails[part] = third(part)
    for part in (1, 0, 2):
        third_finish(part, tails[part])
    for copy in started:
        copy.wait_send()


COPIES = 4 + 12 + 12 + 6 + 18 + 9


def local(design, observed, weight_class, calib_unit, class_weight, calib_scale):
    dense = (ROWS // LANES, LANES)
    vmem = pl.BlockSpec(memory_space=pltpu.VMEM)
    panels = pltpu.VMEM((4, 4, 4, TILE, LANES), F32)
    tile = pl.pallas_call(
        kernel,
        out_shape=jax.ShapeDtypeStruct((TILE, LANES), F32),
        in_specs=[pl.BlockSpec(memory_space=pl.ANY), vmem, vmem, vmem,
                  pl.BlockSpec(memory_space=pltpu.SMEM), vmem],
        out_specs=vmem,
        scratch_shapes=[
            pltpu.VMEM((ROWS, WIDTH), BF16),
            pltpu.VMEM((BLOCKS, LANES, ROWS), BF16),
            pltpu.VMEM((BLOCKS, ROWS), F32),
            pltpu.VMEM((2 * BLOCKS, ROWS), BF16),
            panels, panels, panels,
            pltpu.VMEM((2, 6, 4, PART, LANES), F32),
            pltpu.VMEM((2, 6, 4, PART, LANES), F32),
            pltpu.VMEM((6, 2, 4, PART, LANES), F32),
            pltpu.VMEM((3, 6, 2, PART, LANES), F32),
            pltpu.VMEM((3, 3, PART, LANES), F32),
            pltpu.SemaphoreType.DMA((CHUNKS,)),
            pltpu.SemaphoreType.DMA((COPIES,)),
            pltpu.SemaphoreType.DMA((COPIES,)),
        ],
        compiler_params=pltpu.CompilerParams(
            collective_id=0, has_side_effects=True, vmem_limit_bytes=56 * 2**20
        ),
    )(
        design,
        observed.reshape(dense),
        weight_class.reshape(dense),
        calib_unit.reshape(dense),
        class_weight,
        calib_scale.T,
    )
    row, col = lax.axis_index("rows"), lax.axis_index("grid")
    right_hand = lax.dynamic_slice(tile, (64, 64 * (row % 2) + 8 * col), (1, 8)).reshape(8)
    return tile[:64], right_hand, tile[65, 0]


def solution(mesh):
    both = ("rows", "grid")
    return jax.shard_map(
        local,
        mesh=mesh,
        in_specs=(P(both, None), P(both), P(both), P(both), P(), P()),
        out_specs=(P("rows", "grid"), P(both), P()),
        check_vma=False,
    )
```

time: 106 us -> 45.1 us (0.43); the launches traced: 104 us -> 44.8 us
  blocking collectives: 55 us -> 0 us
  Pallas kernels: 0 us -> 40.4 us
  matrix products: 13.7 us -> 0 us
  starting transfers between devices: 11.5 us -> 0 us
  other arithmetic: 11.2 us -> 0 us
  local copies, waits for them, and re-layouts: 10.4 us -> 3.81 us
  between operations: 2.57 us -> 0.66 us
    psum x4 -> x0, blocking collectives: 46.8 us -> none  [by_axis(): return functools.reduce(lax.psum, axes, shard)]
    pallas_call x0 -> x1, Pallas kernels: none -> 40.4 us  [local(): pl.pallas_call(kernel, out_shape=jax.ShapeDtypeStruct((TILE, LANES), F32)...]
    dot_general x4 -> x0, matrix products: 13.7 us -> none  [the longest x1 6.69 us: local(): jnp.einsum('nra,ngb->rgab', weighted.reshape(row_count, count_rows, band)...]
    all_to_all x1 -> x0, starting transfers between devices: 11.5 us -> none  [sum_by_axis(): lax.all_to_all(nearer, far, split_axis=0, concat_axis=0, tiled=True)]
    unnamed x13 -> x0, local copies, waits for them, and re-layouts: 8.71 us -> none
    all_to_all x1 -> x0, blocking collectives: 8.17 us -> none  [summed_on_arrival(): lax.all_to_all(blocks, axis, split_axis=0, concat_axis=0, tiled=True)]
    convert_element_type x2 -> x0, other arithmetic: 5.15 us -> none  [the longest x1 4.54 us: local(): (root_weight[:, None] * scaled.astype(jnp.float32)).astype(jnp.bfloat16)]
    reduce_sum x2 -> x0, other arithmetic: 4.22 us -> none  [the longest x1 4.08 us: summed_on_arrival(): return arrived.sum(axis=0)]
  transfers between devices with their start and end apart: 1 -> 0, of which waited for: 0 -> 0; matrix products, arithmetic and copies ran while one was open for 6% -> 0% of each run, Pallas kernels for 0% -> 0%
where the time goes in v1:
time: 45.1 us; the launch traced here: 44.8 us
  Pallas kernels  40.4 us (90%)
  local copies, waits for them, and re-layouts  3.81 us (8%)
  between operations  0.66 us (1%)
    pallas_call x1, Pallas kernels, local(): pl.pallas_call(kernel, out_shape=jax.ShapeDtypeStruct((TILE, LANES), F32)...  40.4 us
    slice x2, local copies, waits for them, and re-layouts, local(): return (tile[:64], right_hand, tile[65, 0])  2.56 us
    reshape x1, local copies, waits for them, and re-layouts, local(): lax.dynamic_slice(tile, (64, 64 * (row % 2) + 8 * col), (1, 8)).reshape(8)  1.25 us

profile of v1, /device:TPU:0, one launch (start us, length us, event | category | flops | bytes accessed | tf_op | source)
XLA Modules:
  0.0 44.8 jit_solution(17029611188719723228)
XLA Ops:
  0.6 40.4 %shard_map.85 = f32[72,128]{1,0:T(8,128)} custom-call(bf16[3072,1024]{1,0:T(8,128)(2,1)} %design.1, f32[24,128]{1,0:T(8,128)} %bitcast.7, s32[24,128]{1,0:T(8,128)} %bitcast.8, s32[24,128]{1,0:T(8,128)} %bitcast.9, f32[16]{0:T(128)} %class_weight.1, f32[8,64]{1,0:T(8,128)} %bitcast.10), custom_call_target="tpu_custom_call" | custom-call | tf_op jit(solution)/shard_map/pallas_call | solution.py:295
  41.0 1.2 %slice.7 = f32[1,1]{1,0:T(1,128)} slice(f32[72,128]{1,0:T(8,128)} %shard_map.85), slice={[65:66], [0:1]} | slice | bytes 8 | tf_op jit(solution)/shard_map/slice | solution.py:329
  42.2 1.3 %dynamic-slice_bitcast_fusion = f32[8]{0:T(128)} fusion(f32[72,128]{1,0:T(8,128)} %shard_map.85, s32[]{:T(128)S(6)} %select_n.11), kind=kLoop, calls=%fused_computation | loop fusion | bytes 68 | tf_op jit(solution)/shard_map/reshape | solution.py:328
  43.5 1.4 %slice.6 = f32[64,128]{1,0:T(8,128)} slice(f32[72,128]{1,0:T(8,128)} %shard_map.85), slice={[0:64], [0:128]} | slice | bytes 65536 | tf_op jit(solution)/shard_map/slice | solution.py:329

commit v2 on v0

v2 whole, which is shorter than its diff:
```python
import functools

import jax
import jax.numpy as jnp
from jax import lax
from jax.experimental import pallas as pl
from jax.experimental.pallas import tpu as pltpu
from jax.sharding import PartitionSpec as P

F32 = jnp.float32
BF16 = jnp.bfloat16
ROWS = 3072
WIDTH = 1024
BLOCKS = 8
LANES = 128
UNITS = 64
CLASSES = 16
CHUNK = 256
CHUNKS = ROWS // CHUNK
TILE = 64
STEP = 1024
PARTS = ((0, 24), (24, 16), (40, 24))
EXTRA = 16
TOTAL = 393216.0
OFFSETS = (2, 1, 3, 0)
NT = (((1,), (1,)), ((), ()))
MESH = pl.DeviceIdType.MESH


def part_rows(part):
    return pl.ds(*PARTS[part])


def kernel(
    design, observed_in, class_in, unit_in, weight_in, scale_in,
    out, out_extra,
    dbuf, wt, row_scale, row_obs, own, other, arrived, partial,
    first_xz, first_y, second_0, second_1, second_2, last_0, last_1, last_2,
    extra_core, extra_ring,
    observed, weight_class, calib_unit, class_weight, scale_t,
    load_sem, small_sem, send_sem, recv_sem,
):
    r = lax.axis_index("rows")
    g = lax.axis_index("grid")
    z, x, y, c = r // 4, r % 4, g // 2, g % 2

    small = [
        pltpu.make_async_copy(src, dst, small_sem.at[i])
        for i, (src, dst) in enumerate([
            (class_in, weight_class), (weight_in, class_weight), (observed_in, observed),
            (unit_in, calib_unit), (scale_in, scale_t),
        ])
    ]
    for copy in small:
        copy.start()
    for q in range(CHUNKS):
        rows = pl.ds(q * CHUNK, CHUNK)
        pltpu.make_async_copy(design.at[rows], dbuf.at[rows], load_sem.at[q]).start()

    def device(dz=0, dx=0, dy=0, flip=False):
        core = 1 - c if flip else c
        return (4 * ((z + dz) % 4) + (x + dx) % 4, 2 * ((y + dy) % 4) + core)

    partner = device(flip=True)
    axis_device = {
        "x": lambda d: device(dx=d),
        "z": lambda d: device(dz=d),
        "y": lambda d: device(dy=d),
    }
    barrier = pltpu.get_barrier_semaphore()
    peers = [partner] + [axis_device[a](d) for a in "xzy" for d in (1, 2, 3)]
    for peer in peers:
        pl.semaphore_signal(barrier, inc=1, device_id=peer, device_id_type=MESH)

    started = []

    def send(src, dst, peer):
        index = len(started)
        copy = pltpu.make_async_remote_copy(
            src_ref=src, dst_ref=dst, send_sem=send_sem.at[index],
            recv_sem=recv_sem.at[index], device_id=peer, device_id_type=MESH,
        )
        copy.start()
        started.append(copy)
        return copy

    for copy in small:
        copy.wait()
    classes = weight_class[...]
    row_weight = jnp.zeros(classes.shape, F32)
    for k in range(CLASSES):
        row_weight = jnp.where(classes == k, class_weight[k], row_weight)
    root = jnp.sqrt(row_weight)
    obs = observed[...]
    extra_core[c] = jnp.zeros((EXTRA, LANES), F32) + jnp.sum(row_weight * obs * obs)
    root_obs = root * obs
    unit_id = lax.broadcasted_iota(jnp.int32, (UNITS, LANES), 0)
    scales = scale_t[...]
    obs_line = lax.broadcasted_iota(jnp.int32, (EXTRA, LANES), 0)
    for q in range(ROWS // LANES):
        cols = slice(q * LANES, (q + 1) * LANES)
        hot = (unit_id == calib_unit[q : q + 1, :]).astype(F32)
        scale = jnp.dot(scales, hot, precision=lax.Precision.HIGHEST, preferred_element_type=F32)
        scale = scale * root[q : q + 1, :]
        row_scale[:, cols] = scale
        value = root_obs[q : q + 1, :]
        high = value.astype(BF16).astype(F32)
        both = jnp.where(obs_line == 0, high, jnp.where(obs_line == 1, value - high, 0.0))
        row_obs[:, cols] = both.astype(BF16)

    def block_at(position):
        core = c if position % 2 else 1 - c
        return (y + OFFSETS[position // 2]) % 4, core

    def weigh(q):
        rows = pl.ds(q * CHUNK, CHUNK)
        pltpu.make_async_copy(design.at[rows], dbuf.at[rows], load_sem.at[q]).wait()
        for position in range(BLOCKS):
            high, core = block_at(position)
            block = 2 * high + core
            cols = pl.ds(pl.multiple_of(block * LANES, LANES), LANES)
            piece = dbuf[rows, cols].T.astype(F32)
            wt[position, :, rows] = (piece * row_scale[pl.ds(block, 1), rows]).astype(BF16)

    def store(row_position, col_position, value):
        target = own if col_position % 2 else other
        high, core = block_at(row_position)
        for half in range(2):
            target[col_position // 2, high, 2 * core + half] = value[64 * half : 64 * half + 64]

    def multiply(i, j, cols):
        count = ROWS if cols == slice(None) else STEP
        left = wt[2 * i : 2 * i + 2, :, cols].reshape(2 * LANES, count)
        if i == j:
            left = jnp.concatenate([left, row_obs[:, cols]], axis=0)
        right = wt[2 * j : 2 * j + 2, :, cols].reshape(2 * LANES, count)
        return lax.dot_general(left, right, NT, preferred_element_type=F32)

    def keep(i, j, product):
        for a in range(2):
            for b in range(2):
                value = product[a * LANES : (a + 1) * LANES, b * LANES : (b + 1) * LANES]
                store(2 * i + a, 2 * j + b, value)
                if i > j:
                    store(2 * j + b, 2 * i + a, value.T)
        if i == j:
            line = 2 * LANES
            rhs = product[line : line + 1] + product[line + 1 : line + 2]
            for b in range(2):
                high, core = block_at(2 * j + b)
                extra_core[c, pl.ds(2 * high + core, 1), :] = rhs[:, b * LANES : (b + 1) * LANES]

    def square(i, j):
        keep(i, j, multiply(i, j, slice(None)))

    def panel(k):
        for i in range(k, 4):
            square(i, k)

    def first_panel(step):
        cols = slice(step * STEP, (step + 1) * STEP)
        for i in range(4):
            product = multiply(i, 0, cols)
            lines = product.shape[0]
            if step:
                product = product + partial[i, :lines]
            if (step + 1) * STEP < ROWS:
                partial[i, :lines] = product
            else:
                keep(i, 0, product)

    def exchange(k):
        return send(other.at[k], arrived.at[k], partner)

    def merge(k, copy):
        copy.wait_recv()

        def add(i, _):
            own[k, i] = own[k, i] + arrived[k, i]
            return 0

        lax.fori_loop(0, 4, add, 0)

    def scatter(axis, src, bufs):
        to = axis_device[axis]
        return [(send(src(d), bufs.at[d - 1], to(d)), bufs.at[d - 1]) for d in (2, 1, 3)]

    def gather(src, copies):
        for copy, _ in copies:
            copy.wait_recv()
        mine = src(0)
        total = mine[...]
        for _, buf in copies:
            total = total + buf[...]
        mine[...] = total

    panel_of = {2: 0, 1: 1, 3: 2, 0: 3}

    def at(part, k, dz, dx):
        return own.at[k, dz, dx, part_rows(part), :]

    every = slice(None)

    def src_x(k):
        return lambda d: at(0, k, every, (x + d) % 4)

    def src_z(k):
        return lambda d: at(2, k, (z + d) % 4, every)

    def src_y(d):
        return at(1, panel_of[d], every, every)

    def src_0y(d):
        return at(0, panel_of[d], every, x)

    def src_1z(d):
        return at(1, 3, (z + d) % 4, every)

    def src_2x(k):
        return lambda d: at(2, k, z, (x + d) % 4)

    def src_0z(d):
        return at(0, 3, (z + d) % 4, x)

    def src_1x(d):
        return at(1, 3, z, (x + d) % 4)

    def src_2y(d):
        return at(2, panel_of[d], z, x)

    to_y = axis_device["y"]
    distance_of = (2, 1, 3, 0)
    step_x, step_z, step_y, step_0y, step_2x, step_2y = {}, {}, [], [], {}, []

    def spread(k):
        step_x[k] = scatter("x", src_x(k), first_xz.at[0, k])
        step_z[k] = scatter("z", src_z(k), first_xz.at[1, k])
        if k < 3:
            d = distance_of[k]
            step_y.append((send(src_y(d), first_y.at[k], to_y(d)), first_y.at[k]))

    def gather_extra(stage, copies):
        for copy in copies:
            copy.wait_recv()
        total = extra_ring[stage, 0] + extra_ring[stage, 1]
        return total + extra_ring[stage, 2] + extra_ring[stage, 3]

    def spread_extra(stage, total):
        place = (x, y, z)[stage]
        to = axis_device["xyz"[stage]]
        extra_ring[stage, place] = total
        slot = extra_ring.at[stage, place]
        return [send(slot, slot, to(d)) for d in (2, 1, 3)]

    per_step = STEP // CHUNK
    for step in range(ROWS // STEP + 1):
        if step < ROWS // STEP:
            for q in range(step * per_step, (step + 1) * per_step):
                weigh(q)
        if step:
            first_panel(step - 1)
    pl.semaphore_wait(barrier, len(peers))
    sent_0 = exchange(0)
    panel(1)
    sent_1 = exchange(1)
    panel(2)
    sent_2 = exchange(2)
    merge(0, sent_0)
    spread(0)
    panel(3)
    sent_3 = exchange(3)
    slot = extra_core.at[c]
    sent_extra = send(slot, slot, partner)
    for k, copy in ((1, sent_1), (2, sent_2), (3, sent_3)):
        merge(k, copy)
        spread(k)
    sent_extra.wait_recv()
    extra = spread_extra(0, extra_core[0] + extra_core[1])
    for k in range(4):
        gather(src_x(k), step_x[k])
        if k < 3:
            d = distance_of[k]
            step_0y.append((send(src_0y(d), second_0.at[k], to_y(d)), second_0.at[k]))
        gather(src_z(k), step_z[k])
        step_2x[k] = scatter("x", src_2x(k), second_2.at[k])
    extra = spread_extra(1, gather_extra(0, extra))
    gather(src_y, step_y)
    step_1z = scatter("z", src_1z, second_1)
    gather(src_0y, step_0y)
    step_0z = scatter("z", src_0z, last_0)
    for k in range(4):
        gather(src_2x(k), step_2x[k])
        if k < 3:
            d = distance_of[k]
            step_2y.append((send(src_2y(d), last_2.at[k], to_y(d)), last_2.at[k]))
    extra = spread_extra(2, gather_extra(1, extra))
    gather(src_1z, step_1z)
    step_1x = scatter("x", src_1x, last_1)
    for part, src, copies in ((0, src_0z, step_0z), (2, src_2y, step_2y), (1, src_1x, step_1x)):
        for copy, _ in copies:
            copy.wait_recv()
        total = src(0)[...]
        for _, buf in copies:
            total = total + buf[...]
        out[part_rows(part), :] = total * (1.0 / TOTAL)
    out_extra[...] = gather_extra(2, extra) * (1.0 / TOTAL)
    for copy in started:
        copy.wait_send()


COPIES = 4 + 12 + 12 + 3 + 3 + 3 + 12 + 9 + 10


def local(design, observed, weight_class, calib_unit, class_weight, calib_scale):
    dense = (ROWS // LANES, LANES)
    vmem = pl.BlockSpec(memory_space=pltpu.VMEM)
    panels = pltpu.VMEM((4, 4, 4, TILE, LANES), F32)
    rows_x, rows_y, rows_z = (rows for _, rows in PARTS)
    gram, extra = pl.pallas_call(
        kernel,
        out_shape=(jax.ShapeDtypeStruct((TILE, LANES), F32), jax.ShapeDtypeStruct((EXTRA, LANES), F32)),
        in_specs=[pl.BlockSpec(memory_space=pltpu.HBM)] * 6,
        out_specs=(vmem, vmem),
        scratch_shapes=[
            pltpu.VMEM((ROWS, WIDTH), BF16),
            pltpu.VMEM((BLOCKS, LANES, ROWS), BF16),
            pltpu.VMEM((BLOCKS, ROWS), F32),
            pltpu.VMEM((EXTRA, ROWS), BF16),
            panels, panels, panels,
            pltpu.VMEM((4, 2 * LANES + EXTRA, 2 * LANES), F32),
            pltpu.VMEM((2, 4, 3, 4, rows_x, LANES), F32),
            pltpu.VMEM((3, 4, 4, rows_y, LANES), F32),
            pltpu.VMEM((3, 4, rows_x, LANES), F32),
            pltpu.VMEM((3, 4, rows_y, LANES), F32),
            pltpu.VMEM((4, 3, rows_z, LANES), F32),
            pltpu.VMEM((3, rows_x, LANES), F32),
            pltpu.VMEM((3, rows_y, LANES), F32),
            pltpu.VMEM((3, rows_z, LANES), F32),
            pltpu.VMEM((2, EXTRA, LANES), F32),
            pltpu.VMEM((3, 4, EXTRA, LANES), F32),
            pltpu.VMEM(dense, F32),
            pltpu.VMEM(dense, jnp.int32),
            pltpu.VMEM(dense, jnp.int32),
            pltpu.SMEM((CLASSES,), F32),
            pltpu.VMEM((BLOCKS, UNITS), F32),
            pltpu.SemaphoreType.DMA((CHUNKS,)),
            pltpu.SemaphoreType.DMA((5,)),
            pltpu.SemaphoreType.DMA((COPIES,)),
            pltpu.SemaphoreType.DMA((COPIES,)),
        ],
        compiler_params=pltpu.CompilerParams(
            collective_id=0, has_side_effects=True, vmem_limit_bytes=32 * 2**20
        ),
    )(
        *[pltpu.with_memory_space_constraint(v, pltpu.HBM) for v in (design,
        observed.reshape(dense),
        weight_class.reshape(dense),
        calib_unit.reshape(dense),
        class_weight,
        calib_scale.T)],
    )
    row, col = lax.axis_index("rows"), lax.axis_index("grid")
    right_hand = lax.dynamic_slice(extra, (row // 2, 64 * (row % 2) + 8 * col), (1, 8)).reshape(8)
    return gram, right_hand, extra[BLOCKS, 0]


def solution(mesh):
    both = ("rows", "grid")
    return jax.shard_map(
        local,
        mesh=mesh,
        in_specs=(P(both, None), P(both), P(both), P(both), P(), P()),
        out_specs=(P("rows", "grid"), P(both), P()),
        check_vma=False,
    )
```

time: 106 us -> 38.2 us (0.36); the launches traced: 104 us -> 38.1 us
  blocking collectives: 55 us -> 0 us
  Pallas kernels: 0 us -> 35.7 us
  matrix products: 13.7 us -> 0 us
  starting transfers between devices: 11.5 us -> 0 us
  other arithmetic: 11.2 us -> 0 us
  local copies, waits for them, and re-layouts: 10.4 us -> 1.71 us
  between operations: 2.57 us -> 0.67 us
    psum x4 -> x0, blocking collectives: 46.8 us -> none  [by_axis(): return functools.reduce(lax.psum, axes, shard)]
    pallas_call x0 -> x1, Pallas kernels: none -> 35.7 us  [local(): pl.pallas_call(kernel, out_shape=(jax.ShapeDtypeStruct((TILE, LANES), F32...]
    dot_general x4 -> x0, matrix products: 13.7 us -> none  [the longest x1 6.69 us: local(): jnp.einsum('nra,ngb->rgab', weighted.reshape(row_count, count_rows, band)...]
    all_to_all x1 -> x0, starting transfers between devices: 11.5 us -> none  [sum_by_axis(): lax.all_to_all(nearer, far, split_axis=0, concat_axis=0, tiled=True)]
    all_to_all x1 -> x0, blocking collectives: 8.17 us -> none  [summed_on_arrival(): lax.all_to_all(blocks, axis, split_axis=0, concat_axis=0, tiled=True)]
    unnamed x13 -> x1, local copies, waits for them, and re-layouts: 8.71 us -> 0.61 us
    convert_element_type x2 -> x0, other arithmetic: 5.15 us -> none  [the longest x1 4.54 us: local(): (root_weight[:, None] * scaled.astype(jnp.float32)).astype(jnp.bfloat16)]
    reduce_sum x2 -> x0, other arithmetic: 4.22 us -> none  [the longest x1 4.08 us: summed_on_arrival(): return arrived.sum(axis=0)]
  transfers between devices with their start and end apart: 1 -> 0, of which waited for: 0 -> 0; matrix products, arithmetic and copies ran while one was open for 6% -> 0% of each run, Pallas kernels for 0% -> 0%
where the time goes in v2:
time: 38.2 us; the launch traced here: 38.1 us
  Pallas kernels  35.7 us (93%)
  local copies, waits for them, and re-layouts  1.71 us (4%)
  between operations  0.67 us (2%)
    pallas_call x1, Pallas kernels, local(): pl.pallas_call(kernel, out_shape=(jax.ShapeDtypeStruct((TILE, LANES), F32...  35.7 us

profile of v2, /device:TPU:0, one launch (start us, length us, event | category | flops | bytes accessed | tf_op | source)
XLA Modules:
  0.0 38.1 jit_solution(18268330809226724309)
XLA Ops:
  0.7 35.7 %shard_map.85 = (f32[64,128]{1,0:T(8,128)S(1)}, f32[16,128]{1,0:T(8,128)S(1)}) custom-call(bf16[3072,1024]{1,0:T(8,128)(2,1)} %design.1, f32[24,128]{1,0:T(8,128)} %bitcast.7, s32[24,128]{1,0:T(8,128)} %bitcast.8, s32[24,128]{1,0:T(8,128)} %bitcast.9, f32[16]{0:T(128)} %weight_in.1, f32[8,64]{1,0:T(8,128)} %bitcast.10), custom_call_target="tpu_custom_call" | custom-call | tf_op jit(solution)/shard_map/pallas_call | solution.py:319
  36.4 0.5 %slice.3 = f32[1,1]{1,0:T(1,128)} slice(f32[16,128]{1,0:T(8,128)S(1)} %get-tuple-element.6), slice={[8:9], [0:1]} | slice | bytes 8 | tf_op jit(solution)/shard_map/slice | solution.py:364
  36.9 0.6 %dynamic-slice_bitcast_fusion = f32[8]{0:T(128)} fusion(f32[16,128]{1,0:T(8,128)S(1)} %get-tuple-element.6, s32[]{:T(128)S(6)} %select_n.18, s32[]{:T(128)S(6)} %select_n.20), kind=kLoop, calls=%fused_computation | loop fusion | bytes 72 | tf_op jit(solution)/shard_map/reshape | solution.py:363
  37.5 0.6 %copy.10 = f32[64,128]{1,0:T(8,128)} copy(f32[64,128]{1,0:T(8,128)S(1)} %get-tuple-element.10) | data formatting | bytes 65536

commit v3 on v2

--- a/solution.py
+++ b/solution.py
@@ -15,11 +15,11 @@
 LANES = 128
 UNITS = 64
 CLASSES = 16
-CHUNK = 256
-CHUNKS = ROWS // CHUNK
+LOADS = ((0, 512), (512, 1280), (1792, 1280))
+CHUNKS = len(LOADS)
 TILE = 64
-STEP = 1024
 PARTS = ((0, 24), (24, 16), (40, 24))
+RINGS = 3
 EXTRA = 16
 TOTAL = 393216.0
 OFFSETS = (2, 1, 3, 0)
@@ -35,7 +35,7 @@
     design, observed_in, class_in, unit_in, weight_in, scale_in,
     out, out_extra,
     dbuf, wt, row_scale, row_obs, own, other, arrived, partial,
-    first_xz, first_y, second_0, second_1, second_2, last_0, last_1, last_2,
+    ring_x, ring_z, ring_y, first_x, first_z, second_0, second_1, second_2, last_0, last_1, last_2,
     extra_core, extra_ring,
     observed, weight_class, calib_unit, class_weight, scale_t,
     load_sem, small_sem, send_sem, recv_sem,
@@ -54,7 +54,7 @@
     for copy in small:
         copy.start()
     for q in range(CHUNKS):
-        rows = pl.ds(q * CHUNK, CHUNK)
+        rows = pl.ds(*LOADS[q])
         pltpu.make_async_copy(design.at[rows], dbuf.at[rows], load_sem.at[q]).start()
 
     def device(dz=0, dx=0, dy=0, flip=False):
@@ -74,14 +74,18 @@
 
     started = []
 
-    def send(src, dst, peer):
+    def prepare(src, dst, peer):
         index = len(started)
         copy = pltpu.make_async_remote_copy(
             src_ref=src, dst_ref=dst, send_sem=send_sem.at[index],
             recv_sem=recv_sem.at[index], device_id=peer, device_id_type=MESH,
         )
+        started.append(copy)
+        return copy
+
+    def send(src, dst, peer):
+        copy = prepare(src, dst, peer)
         copy.start()
-        started.append(copy)
         return copy
 
     for copy in small:
@@ -96,11 +100,17 @@
     root_obs = root * obs
     unit_id = lax.broadcasted_iota(jnp.int32, (UNITS, LANES), 0)
     scales = scale_t[...]
+    parts = []
+    for _ in range(3):
+        parts.append(scales.astype(BF16).astype(F32))
+        scales = scales - parts[-1]
+    scales = jnp.concatenate(parts, axis=0).astype(BF16)
     obs_line = lax.broadcasted_iota(jnp.int32, (EXTRA, LANES), 0)
     for q in range(ROWS // LANES):
         cols = slice(q * LANES, (q + 1) * LANES)
-        hot = (unit_id == calib_unit[q : q + 1, :]).astype(F32)
-        scale = jnp.dot(scales, hot, precision=lax.Precision.HIGHEST, preferred_element_type=F32)
+        hot = jnp.where(unit_id == calib_unit[q : q + 1, :], 1.0, 0.0).astype(BF16)
+        triple = jnp.dot(scales, hot, preferred_element_type=F32)
+        scale = triple[:BLOCKS] + triple[BLOCKS : 2 * BLOCKS] + triple[2 * BLOCKS :]
         scale = scale * root[q : q + 1, :]
         row_scale[:, cols] = scale
         value = root_obs[q : q + 1, :]
@@ -113,7 +123,7 @@
         return (y + OFFSETS[position // 2]) % 4, core
 
     def weigh(q):
-        rows = pl.ds(q * CHUNK, CHUNK)
+        rows = pl.ds(*LOADS[q])
         pltpu.make_async_copy(design.at[rows], dbuf.at[rows], load_sem.at[q]).wait()
         for position in range(BLOCKS):
             high, core = block_at(position)
@@ -128,13 +138,23 @@
         for half in range(2):
             target[col_position // 2, high, 2 * core + half] = value[64 * half : 64 * half + 64]
 
-    def multiply(i, j, cols):
-        count = ROWS if cols == slice(None) else STEP
+    squares = [(i, j) for j in range(4) for i in range(j, 4)]
+
+    def multiply(i, j, step):
+        start, count = LOADS[step]
+        cols = slice(start, start + count)
         left = wt[2 * i : 2 * i + 2, :, cols].reshape(2 * LANES, count)
         if i == j:
             left = jnp.concatenate([left, row_obs[:, cols]], axis=0)
         right = wt[2 * j : 2 * j + 2, :, cols].reshape(2 * LANES, count)
-        return lax.dot_general(left, right, NT, preferred_element_type=F32)
+        product = lax.dot_general(left, right, NT, preferred_element_type=F32)
+        place, lines = squares.index((i, j)), product.shape[0]
+        if step:
+            product = product + partial[place, :lines]
+        if step + 1 < CHUNKS:
+            partial[place, :lines] = product
+        else:
+            keep(i, j, product)
 
     def keep(i, j, product):
         for a in range(2):
@@ -150,30 +170,21 @@
                 high, core = block_at(2 * j + b)
                 extra_core[c, pl.ds(2 * high + core, 1), :] = rhs[:, b * LANES : (b + 1) * LANES]
 
-    def square(i, j):
-        keep(i, j, multiply(i, j, slice(None)))
-
-    def panel(k):
+    def panel(k, step=CHUNKS - 1):
         for i in range(k, 4):
-            square(i, k)
-
-    def first_panel(step):
-        cols = slice(step * STEP, (step + 1) * STEP)
+            multiply(i, k, step)
+
+    exchanged = {}
+
+    def exchange(j):
+        pairs = [(j, i) for i in range(j, 4)] + [(i, j) for i in range(j + 1, 4)]
+        for k, i in pairs:
+            line = (y + OFFSETS[i]) % 4
+            exchanged[k, i] = send(other.at[k, line], arrived.at[k, line], partner)
+
+    def merge(k):
         for i in range(4):
-            product = multiply(i, 0, cols)
-            lines = product.shape[0]
-            if step:
-                product = product + partial[i, :lines]
-            if (step + 1) * STEP < ROWS:
-                partial[i, :lines] = product
-            else:
-                keep(i, 0, product)
-
-    def exchange(k):
-        return send(other.at[k], arrived.at[k], partner)
-
-    def merge(k, copy):
-        copy.wait_recv()
+            exchanged[k, i].wait_recv()
 
         def add(i, _):
             own[k, i] = own[k, i] + arrived[k, i]
@@ -183,7 +194,12 @@
 
     def scatter(axis, src, bufs):
         to = axis_device[axis]
-        return [(send(src(d), bufs.at[d - 1], to(d)), bufs.at[d - 1]) for d in (2, 1, 3)]
+        return [(prepare(src(d), bufs.at[d - 1], to(d)), bufs.at[d - 1]) for d in (2, 1, 3)]
+
+    def start(copies):
+        for copy, _ in copies:
+            copy.start()
+        return copies
 
     def gather(src, copies):
         for copy, _ in copies:
@@ -194,6 +210,50 @@
             total = total + buf[...]
         mine[...] = total
 
+    class Ring:
+        def __init__(self, axis, src, bufs):
+            right, left = axis_device[axis](1), axis_device[axis](3)
+            self.src, self.bufs = src, bufs
+            self.hop_a = prepare(src(2, 0), bufs.at[0], right)
+            self.hop_b = prepare(src(2, 1), bufs.at[1], left)
+            self.direct_b = prepare(src(1, 1), bufs.at[3], right)
+            self.direct_a = prepare(src(3, 0), bufs.at[2], left)
+            self.last_a = prepare(bufs.at[0], bufs.at[4], right)
+            self.last_b = prepare(bufs.at[1], bufs.at[5], left)
+            self.next_a, self.next_b = src(1, 0), src(3, 1)
+
+        def start_far(self):
+            self.hop_a.start()
+            self.hop_b.start()
+
+        def start_right(self):
+            self.direct_b.start()
+
+        def start_left(self):
+            self.direct_a.start()
+
+        def start(self):
+            self.start_far()
+            self.start_right()
+            self.start_left()
+
+        def pass_right(self):
+            self.hop_a.wait_recv()
+            self.bufs[0] = self.bufs[0] + self.next_a[...]
+            self.last_a.start()
+
+        def pass_left(self):
+            self.hop_b.wait_recv()
+            self.bufs[1] = self.bufs[1] + self.next_b[...]
+            self.last_b.start()
+
+        def finish(self):
+            for half, direct, via in ((0, self.direct_a, self.last_a), (1, self.direct_b, self.last_b)):
+                direct.wait_recv()
+                via.wait_recv()
+                mine = self.src(0, half)
+                mine[...] = mine[...] + self.bufs[2 + half] + self.bufs[4 + half]
+
     panel_of = {2: 0, 1: 1, 3: 2, 0: 3}
 
     def at(part, k, dz, dx):
@@ -201,15 +261,24 @@
 
     every = slice(None)
 
+    def two(half):
+        return pl.ds(2 * half, 2)
+
+    def half_x(k):
+        return lambda d, half: at(0, k, two(half), (x + d) % 4)
+
+    def half_z(k):
+        return lambda d, half: at(2, k, (z + d) % 4, two(half))
+
+    def half_y(d, half):
+        return at(1, panel_of[d], two(half), every)
+
     def src_x(k):
         return lambda d: at(0, k, every, (x + d) % 4)
 
     def src_z(k):
         return lambda d: at(2, k, (z + d) % 4, every)
 
-    def src_y(d):
-        return at(1, panel_of[d], every, every)
-
     def src_0y(d):
         return at(0, panel_of[d], every, x)
 
@@ -230,14 +299,43 @@
 
     to_y = axis_device["y"]
     distance_of = (2, 1, 3, 0)
-    step_x, step_z, step_y, step_0y, step_2x, step_2y = {}, {}, [], [], {}, []
+    step_0y, step_2x, step_2y = [], {}, []
+    rings = {k: (Ring("x", half_x(k), ring_x.at[k]), Ring("z", half_z(k), ring_z.at[k])) for k in range(RINGS)}
+    ring_of_y = Ring("y", half_y, ring_y)
+
+    step_x = {k: scatter("x", src_x(k), first_x.at[k - RINGS]) for k in range(RINGS, 4)}
+    step_z = {k: scatter("z", src_z(k), first_z.at[k - RINGS]) for k in range(RINGS, 4)}
 
     def spread(k):
-        step_x[k] = scatter("x", src_x(k), first_xz.at[0, k])
-        step_z[k] = scatter("z", src_z(k), first_xz.at[1, k])
-        if k < 3:
-            d = distance_of[k]
-            step_y.append((send(src_y(d), first_y.at[k], to_y(d)), first_y.at[k]))
+        if k < RINGS:
+            for ring in rings[k]:
+                ring.start()
+        else:
+            start(step_x[k])
+            start(step_z[k])
+        if k == 0:
+            ring_of_y.start_far()
+        if k == 1:
+            ring_of_y.start_right()
+        if k == 2:
+            ring_of_y.start_left()
+
+    def pass_on(k):
+        for ring in rings[k]:
+            ring.pass_right()
+            ring.pass_left()
+
+    def finish_x(k):
+        if k < RINGS:
+            rings[k][0].finish()
+        else:
+            gather(src_x(k), step_x[k])
+
+    def finish_z(k):
+        if k < RINGS:
+            rings[k][1].finish()
+        else:
+            gather(src_z(k), step_z[k])
 
     def gather_extra(stage, copies):
         for copy in copies:
@@ -252,42 +350,49 @@
         slot = extra_ring.at[stage, place]
         return [send(slot, slot, to(d)) for d in (2, 1, 3)]
 
-    per_step = STEP // CHUNK
-    for step in range(ROWS // STEP + 1):
-        if step < ROWS // STEP:
-            for q in range(step * per_step, (step + 1) * per_step):
-                weigh(q)
-        if step:
-            first_panel(step - 1)
+    weigh(0)
+    for step in range(1, CHUNKS):
+        weigh(step)
+        for k in range(4):
+            panel(k, step - 1)
+    panel(0)
     pl.semaphore_wait(barrier, len(peers))
-    sent_0 = exchange(0)
+    exchange(0)
     panel(1)
-    sent_1 = exchange(1)
+    exchange(1)
     panel(2)
-    sent_2 = exchange(2)
-    merge(0, sent_0)
-    spread(0)
+    exchange(2)
     panel(3)
-    sent_3 = exchange(3)
+    exchange(3)
     slot = extra_core.at[c]
     sent_extra = send(slot, slot, partner)
-    for k, copy in ((1, sent_1), (2, sent_2), (3, sent_3)):
-        merge(k, copy)
-        spread(k)
+    merge(0)
+    spread(0)
+    merge(1)
+    spread(1)
+    merge(2)
+    spread(2)
+    pass_on(0)
+    merge(3)
+    spread(3)
+    ring_of_y.pass_right()
+    ring_of_y.pass_left()
+    for k in range(1, RINGS):
+        pass_on(k)
     sent_extra.wait_recv()
     extra = spread_extra(0, extra_core[0] + extra_core[1])
     for k in range(4):
-        gather(src_x(k), step_x[k])
+        finish_x(k)
         if k < 3:
             d = distance_of[k]
             step_0y.append((send(src_0y(d), second_0.at[k], to_y(d)), second_0.at[k]))
-        gather(src_z(k), step_z[k])
-        step_2x[k] = scatter("x", src_2x(k), second_2.at[k])
+        finish_z(k)
+        step_2x[k] = start(scatter("x", src_2x(k), second_2.at[k]))
     extra = spread_extra(1, gather_extra(0, extra))
-    gather(src_y, step_y)
-    step_1z = scatter("z", src_1z, second_1)
+    ring_of_y.finish()
+    step_1z = start(scatter("z", src_1z, second_1))
     gather(src_0y, step_0y)
-    step_0z = scatter("z", src_0z, last_0)
+    step_0z = start(scatter("z", src_0z, last_0))
     for k in range(4):
         gather(src_2x(k), step_2x[k])
         if k < 3:
@@ -295,7 +400,7 @@
             step_2y.append((send(src_2y(d), last_2.at[k], to_y(d)), last_2.at[k]))
     extra = spread_extra(2, gather_extra(1, extra))
     gather(src_1z, step_1z)
-    step_1x = scatter("x", src_1x, last_1)
+    step_1x = start(scatter("x", src_1x, last_1))
     for part, src, copies in ((0, src_0z, step_0z), (2, src_2y, step_2y), (1, src_1x, step_1x)):
         for copy, _ in copies:
             copy.wait_recv()
@@ -308,7 +413,7 @@
         copy.wait_send()
 
 
-COPIES = 4 + 12 + 12 + 3 + 3 + 3 + 12 + 9 + 10
+COPIES = 16 + 2 * (6 * RINGS + 3 * (4 - RINGS)) + 6 + 3 + 3 + 12 + 9 + 10
 
 
 def local(design, observed, weight_class, calib_unit, class_weight, calib_scale):
@@ -327,9 +432,12 @@
             pltpu.VMEM((BLOCKS, ROWS), F32),
             pltpu.VMEM((EXTRA, ROWS), BF16),
             panels, panels, panels,
-            pltpu.VMEM((4, 2 * LANES + EXTRA, 2 * LANES), F32),
-            pltpu.VMEM((2, 4, 3, 4, rows_x, LANES), F32),
-            pltpu.VMEM((3, 4, 4, rows_y, LANES), F32),
+            pltpu.VMEM((10, 2 * LANES + EXTRA, 2 * LANES), F32),
+            pltpu.VMEM((RINGS, 6, 2, rows_x, LANES), F32),
+            pltpu.VMEM((RINGS, 6, 2, rows_z, LANES), F32),
+            pltpu.VMEM((6, 2, 4, rows_y, LANES), F32),
+            pltpu.VMEM((4 - RINGS, 3, 4, rows_x, LANES), F32),
+            pltpu.VMEM((4 - RINGS, 3, 4, rows_z, LANES), F32),
             pltpu.VMEM((3, 4, rows_x, LANES), F32),
             pltpu.VMEM((3, 4, rows_y, LANES), F32),
             pltpu.VMEM((4, 3, rows_z, LANES), F32),

time: 38.2 us -> 34.8 us (0.911)
  Pallas kernels: 35.7 us -> 32.2 us
    pallas_call x1, Pallas kernels: 35.7 us -> 32.2 us  [local(): pl.pallas_call(kernel, out_shape=(jax.ShapeDtypeStruct((TILE, LANES), F32...]
where the time goes in v3:
time: 34.8 us; the launch traced here: 34.6 us
  Pallas kernels  32.2 us (93%)
  local copies, waits for them, and re-layouts  1.71 us (5%)
  between operations  0.67 us (2%)
    pallas_call x1, Pallas kernels, local(): pl.pallas_call(kernel, out_shape=(jax.ShapeDtypeStruct((TILE, LANES), F32...  32.2 us

profile of v3, /device:TPU:0, one launch (start us, length us, event | category | flops | bytes accessed | tf_op | source)
XLA Modules:
  0.0 34.6 jit_solution(4329373042402458914)
XLA Ops:
  0.7 32.2 %shard_map.85 = (f32[64,128]{1,0:T(8,128)S(1)}, f32[16,128]{1,0:T(8,128)S(1)}) custom-call(bf16[3072,1024]{1,0:T(8,128)(2,1)} %design.1, f32[24,128]{1,0:T(8,128)} %bitcast.7, s32[24,128]{1,0:T(8,128)} %bitcast.8, s32[24,128]{1,0:T(8,128)} %bitcast.9, f32[16]{0:T(128)} %weight_in.1, f32[8,64]{1,0:T(8,128)} %bitcast.10), custom_call_target="tpu_custom_call" | custom-call | tf_op jit(solution)/shard_map/pallas_call | solution.py:424
  32.9 0.5 %slice.3 = f32[1,1]{1,0:T(1,128)} slice(f32[16,128]{1,0:T(8,128)S(1)} %get-tuple-element.6), slice={[8:9], [0:1]} | slice | bytes 8 | tf_op jit(solution)/shard_map/slice | solution.py:472
  33.4 0.6 %dynamic-slice_bitcast_fusion = f32[8]{0:T(128)} fusion(f32[16,128]{1,0:T(8,128)S(1)} %get-tuple-element.6, s32[]{:T(128)S(6)} %select_n.18, s32[]{:T(128)S(6)} %select_n.20), kind=kLoop, calls=%fused_computation | loop fusion | bytes 72 | tf_op jit(solution)/shard_map/reshape | solution.py:471
  34.0 0.6 %copy.10 = f32[64,128]{1,0:T(8,128)} copy(f32[64,128]{1,0:T(8,128)S(1)} %get-tuple-element.10) | data formatting | bytes 65536

commit v4 on v3

--- a/solution.py
+++ b/solution.py
@@ -413,6 +413,15 @@
         copy.wait_send()
 
 
+def split(gram, extra, out_gram, out_rhs, out_chi):
+    r, g = lax.axis_index("rows"), lax.axis_index("grid")
+    out_gram[...] = gram[...]
+    line = extra[pl.ds(r // 2, 1), :]
+    line = pltpu.roll(line, (2 * LANES - (64 * (r % 2) + 8 * g)) % LANES, 1)
+    out_rhs[...] = line[0, :8]
+    out_chi[0] = extra[BLOCKS, 0]
+
+
 COPIES = 16 + 2 * (6 * RINGS + 3 * (4 - RINGS)) + 6 + 3 + 3 + 12 + 9 + 10
 
 
@@ -467,9 +476,18 @@
         class_weight,
         calib_scale.T)],
     )
-    row, col = lax.axis_index("rows"), lax.axis_index("grid")
-    right_hand = lax.dynamic_slice(extra, (row // 2, 64 * (row % 2) + 8 * col), (1, 8)).reshape(8)
-    return gram, right_hand, extra[BLOCKS, 0]
+    gram, right_hand, chi = pl.pallas_call(
+        split,
+        out_shape=(
+            jax.ShapeDtypeStruct((TILE, LANES), F32),
+            jax.ShapeDtypeStruct((8,), F32),
+            jax.ShapeDtypeStruct((1,), F32),
+        ),
+        in_specs=[vmem, vmem],
+        out_specs=(vmem, vmem, pl.BlockSpec(memory_space=pltpu.SMEM)),
+        compiler_params=pltpu.CompilerParams(vmem_limit_bytes=2**20),
+    )(gram, extra)
+    return gram, right_hand, chi.reshape(())
 
 
 def solution(mesh):

time: 34.8 us -> 33.6 us (0.966)
  local copies, waits for them, and re-layouts: 1.71 us -> 0 us
  Pallas kernels: 32.2 us -> 32.9 us
    pallas_call x0 -> x1, Pallas kernels: none -> 0.65 us  [local(): pl.pallas_call(split, out_shape=(jax.ShapeDtypeStruct((TILE, LANES), F32)...]
    unnamed x1 -> x0, local copies, waits for them, and re-layouts: 0.61 us -> none
    reshape x1 -> x0, local copies, waits for them, and re-layouts: 0.58 us -> none  [local(): lax.dynamic_slice(extra, (row // 2, 64 * (row % 2) + 8 * col), (1, 8))]
    slice x1 -> x0, local copies, waits for them, and re-layouts: 0.51 us -> none  [local(): return (gram, right_hand, extra[BLOCKS, 0])]
where the time goes in v4:
time: 33.6 us; the launch traced here: 33.5 us
  Pallas kernels  32.9 us (98%)
  between operations  0.64 us (2%)
    pallas_call x1, Pallas kernels, local(): pl.pallas_call(kernel, out_shape=(jax.ShapeDtypeStruct((TILE, LANES), F32...  32.2 us

profile of v4, /device:TPU:0, one launch (start us, length us, event | category | flops | bytes accessed | tf_op | source)
XLA Modules:
  0.0 33.5 jit_solution(16777900944558445174)
XLA Ops:
  0.6 32.2 %shard_map.85 = (f32[64,128]{1,0:T(8,128)S(1)}, f32[16,128]{1,0:T(8,128)S(1)}) custom-call(bf16[3072,1024]{1,0:T(8,128)(2,1)} %design.1, f32[24,128]{1,0:T(8,128)} %bitcast.5, s32[24,128]{1,0:T(8,128)} %bitcast.6, s32[24,128]{1,0:T(8,128)} %bitcast.7, f32[16]{0:T(128)} %weight_in.1, f32[8,64]{1,0:T(8,128)} %bitcast.8), custom_call_target="tpu_custom_call" | custom-call | tf_op jit(solution)/shard_map/pallas_call | solution.py:433
  32.8 0.6 %shard_map.86 = (f32[64,128]{1,0:T(8,128)}, f32[8]{0:T(128)}, f32[1]{0:T(128)}) custom-call(f32[64,128]{1,0:T(8,128)S(1)} %get-tuple-element.8.gram, f32[16,128]{1,0:T(8,128)S(1)} %get-tuple-element.9.extra), custom_call_target="tpu_custom_call" | custom-call | tf_op jit(solution)/shard_map/pallas_call | solution.py:479

commit v5 on v4

--- a/solution.py
+++ b/solution.py
@@ -381,16 +381,21 @@
         pass_on(k)
     sent_extra.wait_recv()
     extra = spread_extra(0, extra_core[0] + extra_core[1])
-    for k in range(4):
+    def finish(k):
         finish_x(k)
         if k < 3:
             d = distance_of[k]
             step_0y.append((send(src_0y(d), second_0.at[k], to_y(d)), second_0.at[k]))
         finish_z(k)
         step_2x[k] = start(scatter("x", src_2x(k), second_2.at[k]))
-    extra = spread_extra(1, gather_extra(0, extra))
+
+    finish(0)
+    finish(1)
     ring_of_y.finish()
     step_1z = start(scatter("z", src_1z, second_1))
+    finish(2)
+    finish(3)
+    extra = spread_extra(1, gather_extra(0, extra))
     gather(src_0y, step_0y)
     step_0z = start(scatter("z", src_0z, last_0))
     for k in range(4):

time: 33.6 us -> 33.6 us (level)
  no operation moved by 1% of the time
where the time goes in v5:
time: 33.6 us; the launch traced here: 33.5 us
  Pallas kernels  32.9 us (98%)
  between operations  0.64 us (2%)
    pallas_call x1, Pallas kernels, local(): pl.pallas_call(kernel, out_shape=(jax.ShapeDtypeStruct((TILE, LANES), F32...  32.2 us

profile of v5, /device:TPU:0, one launch (start us, length us, event | category | flops | bytes accessed | tf_op | source)
XLA Modules:
  0.0 33.5 jit_solution(13517083289848120552)
XLA Ops:
  0.6 32.2 %shard_map.85 = (f32[64,128]{1,0:T(8,128)S(1)}, f32[16,128]{1,0:T(8,128)S(1)}) custom-call(bf16[3072,1024]{1,0:T(8,128)(2,1)} %design.1, f32[24,128]{1,0:T(8,128)} %bitcast.5, s32[24,128]{1,0:T(8,128)} %bitcast.6, s32[24,128]{1,0:T(8,128)} %bitcast.7, f32[16]{0:T(128)} %weight_in.1, f32[8,64]{1,0:T(8,128)} %bitcast.8), custom_call_target="tpu_custom_call" | custom-call | tf_op jit(solution)/shard_map/pallas_call | solution.py:438
  32.8 0.6 %shard_map.86 = (f32[64,128]{1,0:T(8,128)}, f32[8]{0:T(128)}, f32[1]{0:T(128)}) custom-call(f32[64,128]{1,0:T(8,128)S(1)} %get-tuple-element.8.gram, f32[16,128]{1,0:T(8,128)S(1)} %get-tuple-element.9.extra), custom_call_target="tpu_custom_call" | custom-call | tf_op jit(solution)/shard_map/pallas_call | solution.py:484

commit v6 on v5

--- a/solution.py
+++ b/solution.py
@@ -363,15 +363,17 @@
     panel(2)
     exchange(2)
     panel(3)
-    exchange(3)
     slot = extra_core.at[c]
     sent_extra = send(slot, slot, partner)
+    exchange(3)
     merge(0)
     spread(0)
     merge(1)
     spread(1)
     merge(2)
     spread(2)
+    sent_extra.wait_recv()
+    extra = spread_extra(0, extra_core[0] + extra_core[1])
     pass_on(0)
     merge(3)
     spread(3)
@@ -379,8 +381,6 @@
     ring_of_y.pass_left()
     for k in range(1, RINGS):
         pass_on(k)
-    sent_extra.wait_recv()
-    extra = spread_extra(0, extra_core[0] + extra_core[1])
     def finish(k):
         finish_x(k)
         if k < 3:
@@ -389,13 +389,14 @@
         finish_z(k)
         step_2x[k] = start(scatter("x", src_2x(k), second_2.at[k]))
 
+    extra = spread_extra(1, gather_extra(0, extra))
     finish(0)
     finish(1)
     ring_of_y.finish()
     step_1z = start(scatter("z", src_1z, second_1))
+    extra = spread_extra(2, gather_extra(1, extra))
     finish(2)
     finish(3)
-    extra = spread_extra(1, gather_extra(0, extra))
     gather(src_0y, step_0y)
     step_0z = start(scatter("z", src_0z, last_0))
     for k in range(4):
@@ -403,7 +404,6 @@
         if k < 3:
             d = distance_of[k]
             step_2y.append((send(src_2y(d), last_2.at[k], to_y(d)), last_2.at[k]))
-    extra = spread_extra(2, gather_extra(1, extra))
     gather(src_1z, step_1z)
     step_1x = start(scatter("x", src_1x, last_1))
     for part, src, copies in ((0, src_0z, step_0z), (2, src_2y, step_2y), (1, src_1x, step_1x)):

time: 33.6 us -> 33.2 us (0.988)
  Pallas kernels: 32.9 us -> 32.4 us
    pallas_call x1, Pallas kernels: 32.2 us -> 31.7 us  [local(): pl.pallas_call(kernel, out_shape=(jax.ShapeDtypeStruct((TILE, LANES), F32...]
where the time goes in v6:
time: 33.2 us; the launch traced here: 33 us
  Pallas kernels  32.4 us (98%)
  between operations  0.64 us (2%)
    pallas_call x1, Pallas kernels, local(): pl.pallas_call(kernel, out_shape=(jax.ShapeDtypeStruct((TILE, LANES), F32...  31.7 us

profile of v6, /device:TPU:0, one launch (start us, length us, event | category | flops | bytes accessed | tf_op | source)
XLA Modules:
  0.0 33.0 jit_solution(2803085662131322226)
XLA Ops:
  0.6 31.7 %shard_map.85 = (f32[64,128]{1,0:T(8,128)S(1)}, f32[16,128]{1,0:T(8,128)S(1)}) custom-call(bf16[3072,1024]{1,0:T(8,128)(2,1)} %design.1, f32[24,128]{1,0:T(8,128)} %bitcast.5, s32[24,128]{1,0:T(8,128)} %bitcast.6, s32[24,128]{1,0:T(8,128)} %bitcast.7, f32[16]{0:T(128)} %weight_in.1, f32[8,64]{1,0:T(8,128)} %bitcast.8), custom_call_target="tpu_custom_call" | custom-call | tf_op jit(solution)/shard_map/pallas_call | solution.py:438
  32.4 0.6 %shard_map.86 = (f32[64,128]{1,0:T(8,128)}, f32[8]{0:T(128)}, f32[1]{0:T(128)}) custom-call(f32[64,128]{1,0:T(8,128)S(1)} %get-tuple-element.8.gram, f32[16,128]{1,0:T(8,128)S(1)} %get-tuple-element.9.extra), custom_call_target="tpu_custom_call" | custom-call | tf_op jit(solution)/shard_map/pallas_call | solution.py:484
